TPU v7x, 32 devices: a whole 2x2x4 slice. The times are simulated.
32 devices in a mesh: rows: 8 (over z, y), grp: 4 (over x, core).
Axes of the slice: x: 2, y: 2, z: 4, core: 2. Of those that a mesh axis runs over, the one named last changes fastest.
Arguments:
- basis: float32 [32, 65536], P(None, ('rows', 'grp')), may hold values from -0.03125 to 0.03125, as said below
- core: float32 [32, 32], replicated, may hold values from -0.3 to 4
- snapshots: bfloat16 [4, 32, 65536], P(None, 'grp', 'rows'), may hold values from -16 to 16
Outputs:
- new_basis: float32 [32, 65536], P(None, ('rows', 'grp'))
- new_core: float32 [32, 32], replicated
- first_coeffs: float32 [4, 32, 32], replicated
Inputs may be any that keep to these rules, and one draw needn't show every extreme that they name: `basis`: rows orthonormal up to float32 rounding.
All inputs are finite; a program needn't handle non-finite values.
Results may differ from a plain program's by a relative error of at most 0.0003.
Values may be sent and summed in bfloat16 or wider, within the bound.
A program may use at most 64 MiB of HBM per device.

v0:
```python
import jax
import jax.numpy as jnp
from jax import lax
from jax.sharding import PartitionSpec as P

BATCHES = 4
epsilon = 1e-06


def contract_rows(left, right):
    return lax.dot_general(
        left,
        right,
        (((1,), (1,)), ((), ())),
        precision=lax.Precision.HIGHEST,
        preferred_element_type=jnp.float32,
    )


def matmul(left, right):
    return jnp.dot(left, right, precision=lax.Precision.HIGHEST, preferred_element_type=jnp.float32)


def lower_solve(factor, right):
    return lax.linalg.triangular_solve(factor, right, left_side=True, lower=True)


def small_update(core_now, total, lower):
    rank = core_now.shape[0]
    cols = lower.shape[0]
    top = jnp.concatenate([core_now, total], axis=1)
    bottom = jnp.concatenate([jnp.zeros((cols, rank), jnp.float32), lower.T], axis=1)
    stacked = jnp.concatenate([top, bottom], axis=0)
    moment = matmul(stacked, stacked.T)
    leading = moment[:, :rank]
    factor = jnp.linalg.cholesky(matmul(leading.T, leading))
    rotation = lower_solve(factor, leading.T).T
    fresh_core = jnp.linalg.cholesky(matmul(rotation.T, matmul(moment, rotation)))
    return (rotation, fresh_core)


def body(basis, core, snapshots):
    rank = basis.shape[0]
    basis_now = basis
    core_now = core
    firsts = []
    gram_basis = lax.psum(contract_rows(basis_now, basis_now), ("rows", "grp"))
    for batch in range(BATCHES):
        columns = lax.all_to_all(snapshots[batch], "grp", split_axis=1, concat_axis=0, tiled=True)
        raw = columns.astype(jnp.float32)
        raw_cross, raw_gram = lax.psum(
            (contract_rows(basis_now, raw), contract_rows(raw, raw)), ("rows", "grp")
        )
        inverse = lax.rsqrt(jnp.diagonal(raw_gram) + epsilon)
        scaled = raw * inverse[:, None]
        cross = raw_cross * inverse[None, :]
        gram_raw = raw_gram * inverse[:, None] * inverse[None, :]
        second = cross - matmul(gram_basis, cross)
        total = cross + second
        basis_cross = cross - matmul(gram_basis, total)
        gram = (
            gram_raw
            - matmul(total.T, cross)
            - matmul(cross.T, total)
            + matmul(total.T, matmul(gram_basis, total))
        )
        twice = scaled - matmul(total.T, basis_now)
        lower = jnp.linalg.cholesky(gram)
        fresh = lower_solve(lower, twice)
        rotation, core_now = small_update(core_now, total, lower)
        cross_fresh = lower_solve(lower, basis_cross.T).T
        halfway = lower_solve(lower, gram)
        gram_fresh = lower_solve(lower, halfway.T).T
        upper_block = jnp.concatenate([gram_basis, cross_fresh], axis=1)
        lower_block = jnp.concatenate([cross_fresh.T, gram_fresh], axis=1)
        combined = jnp.concatenate([upper_block, lower_block], axis=0)
        gram_basis = matmul(rotation.T, matmul(combined, rotation))
        firsts.append(cross)
        basis_now = matmul(rotation[:rank].T, basis_now) + matmul(rotation[rank:].T, fresh)
    return (basis_now, core_now, jnp.stack(firsts, axis=0))


def solution(mesh):
    return jax.shard_map(
        body,
        mesh=mesh,
        in_specs=(P(None, ("rows", "grp")), P(), P(None, "grp", "rows")),
        out_specs=(P(None, ("rows", "grp")), P(), P()),
        check_vma=False,
    )
```

profile of v0, /device:TPU:0, one launch (start us, length us, event | category | flops | bytes accessed | tf_op | source)
XLA Modules:
  0.0 283.6 jit_solution(1562950860485663812)
XLA Ops:
  0.6 1.9 fusion.229
  2.6 4.4 %all-to-all-start = ((bf16[8,4,2048]{2,0,1:T(8,128)(2,1)}), bf16[8,4,2048]{2,0,1:T(8,128)(2,1)S(1)}, u32[]{:S(2)}, u32[]{:S(2)}) async-start(bf16[8,4,2048]{2,0,1:T(8,128)(2,1)} %bitcast), calls=%async_computation | async-start | bytes 262144 | tf_op jit(solution)/shard_map/all_to_all | solution.py:49
  7.4 4.1 %all-to-all-done = bf16[8,4,2048]{2,0,1:T(8,128)(2,1)S(1)} async-done(((bf16[8,4,2048]{2,0,1:T(8,128)(2,1)}), bf16[8,4,2048]{2,0,1:T(8,128)(2,1)S(1)}, u32[]{:S(2)}, u32[]{:S(2)}) %all-to-all-start) | async-done | bytes 131104 | tf_op jit(solution)/shard_map/all_to_all | solution.py:49
  11.6 3.3 %all-to-all-start.1 = ((bf16[8,4,2048]{2,0,1:T(8,128)(2,1)}), bf16[8,4,2048]{2,0,1:T(8,128)(2,1)S(1)}, u32[]{:S(2)}, u32[]{:S(2)}) async-start(bf16[8,4,2048]{2,0,1:T(8,128)(2,1)} %bitcast.15), calls=%async_computation.1 | async-start | bytes 262144 | tf_op jit(solution)/shard_map/all_to_all | solution.py:49
  15.3 42.1 %all-reduce.7 = (f32[32,32]{1,0:T(8,128)S(1)}, f32[32,32]{0,1:T(8,128)S(1)}, f32[32,32]{0,1:T(8,128)S(1)}) all-reduce(f32[32,32]{1,0:T(8,128)S(1)} %fusion.230, f32[32,32]{0,1:T(8,128)S(1)} %fusion.18, f32[32,32]{0,1:T(8,128)S(1)} %fusion.16), channel_id=1, replica_groups=mesh['rows'=8,'grp'=4] {'rows','grp'}, use_global_device_ids=true, to_apply=%region_2.0 | all-reduce | flops 3072 | bytes 24576 | tf_op jit(solution)/shard_map/psum | solution.py:47
  57.4 0.7 gather_fusion
  59.3 2.9 %cholesky.194 = f32[32,32]{1,0:T(8,128)S(1)} custom-call(f32[32,32]{1,0:T(8,128)S(1)} %fusion.134), custom_call_target="Cholesky" | custom-call | tf_op jit(solution)/shard_map/jit(cholesky)/cholesky | solution.py:68
  62.9 0.7 fusion.143
  63.6 2.4 custom-call.34
  67.2 2.9 %cholesky.205 = f32[32,32]{1,0:T(8,128)S(1)} custom-call(f32[32,32]{1,0:T(8,128)S(1)} %fusion.133), custom_call_target="Cholesky" | custom-call | tf_op jit(solution)/shard_map/jit(cholesky)/cholesky | solution.py:36
  70.8 0.7 fusion.64
  71.4 2.4 custom-call.33
  76.5 3.5 %all-to-all-start.2 = ((bf16[8,4,2048]{2,0,1:T(8,128)(2,1)}), bf16[8,4,2048]{2,0,1:T(8,128)(2,1)S(1)}, u32[]{:S(2)}, u32[]{:S(2)}) async-start(bf16[8,4,2048]{2,0,1:T(8,128)(2,1)} %bitcast.39), calls=%async_computation.2 | async-start | bytes 262144 | tf_op jit(solution)/shard_map/all_to_all | solution.py:49
  80.4 41.5 %all-reduce.6 = (f32[32,32]{0,1:T(8,128)S(1)}, f32[32,32]{0,1:T(8,128)S(1)}) all-reduce(f32[32,32]{0,1:T(8,128)S(1)} %fusion.14, f32[32,32]{0,1:T(8,128)S(1)} %fusion.12), channel_id=1, replica_groups=mesh['rows'=8,'grp'=4] {'rows','grp'}, use_global_device_ids=true, to_apply=%region_5.9 | all-reduce | flops 2048 | bytes 16384 | tf_op jit(solution)/shard_map/psum | solution.py:51
  121.9 0.7 gather_fusion.1
  123.5 2.9 %cholesky.216 = f32[32,32]{1,0:T(8,128)S(1)} custom-call(f32[32,32]{1,0:T(8,128)S(1)} %fusion.129), custom_call_target="Cholesky" | custom-call | tf_op jit(solution)/shard_map/jit(cholesky)/cholesky | solution.py:38
  127.3 0.6 fusion.163
  128.5 2.9 %cholesky.227 = f32[32,32]{1,0:T(8,128)S(1)} custom-call(f32[32,32]{1,0:T(8,128)S(1)} %fusion.121), custom_call_target="Cholesky" | custom-call | tf_op jit(solution)/shard_map/jit(cholesky)/cholesky | solution.py:68
  132.1 0.7 fusion.144
  132.8 2.4 custom-call.39
  136.4 2.9 %cholesky.238 = f32[32,32]{1,0:T(8,128)S(1)} custom-call(f32[32,32]{1,0:T(8,128)S(1)} %fusion.120), custom_call_target="Cholesky" | custom-call | tf_op jit(solution)/shard_map/jit(cholesky)/cholesky | solution.py:36
  140.0 0.7 fusion.65
  140.7 2.4 custom-call.38
  145.7 3.5 %all-to-all-start.3 = ((bf16[8,4,2048]{2,0,1:T(8,128)(2,1)}), bf16[8,4,2048]{2,0,1:T(8,128)(2,1)S(1)}, u32[]{:S(2)}, u32[]{:S(2)}) async-start(bf16[8,4,2048]{2,0,1:T(8,128)(2,1)} %bitcast.63), calls=%async_computation.3 | async-start | bytes 262144 | tf_op jit(solution)/shard_map/all_to_all | solution.py:49
  149.7 40.7 %all-reduce.5 = (f32[32,32]{0,1:T(8,128)S(1)}, f32[32,32]{0,1:T(8,128)S(1)}) all-reduce(f32[32,32]{0,1:T(8,128)S(1)} %fusion.10, f32[32,32]{0,1:T(8,128)S(1)} %fusion.8), channel_id=1, replica_groups=mesh['rows'=8,'grp'=4] {'rows','grp'}, use_global_device_ids=true, to_apply=%region_7.12 | all-reduce | flops 2048 | bytes 16384 | tf_op jit(solution)/shard_map/psum | solution.py:51
  190.4 0.7 gather_fusion.2
  192.0 2.9 %cholesky.249 = f32[32,32]{1,0:T(8,128)S(1)} custom-call(f32[32,32]{1,0:T(8,128)S(1)} %fusion.116), custom_call_target="Cholesky" | custom-call | tf_op jit(solution)/shard_map/jit(cholesky)/cholesky | solution.py:38
  195.7 0.6 fusion.164
  197.0 2.9 %cholesky.260 = f32[32,32]{1,0:T(8,128)S(1)} custom-call(f32[32,32]{1,0:T(8,128)S(1)} %fusion.108), custom_call_target="Cholesky" | custom-call | tf_op jit(solution)/shard_map/jit(cholesky)/cholesky | solution.py:68
  200.6 0.7 fusion.142
  201.2 2.4 custom-call.44
  204.8 2.9 %cholesky.271 = f32[32,32]{1,0:T(8,128)S(1)} custom-call(f32[32,32]{1,0:T(8,128)S(1)} %fusion.107), custom_call_target="Cholesky" | custom-call | tf_op jit(solution)/shard_map/jit(cholesky)/cholesky | solution.py:36
  208.5 0.7 fusion.66
  209.1 2.4 custom-call.43
  214.6 39.8 %all-reduce.4 = (f32[32,32]{0,1:T(8,128)S(1)}, f32[32,32]{0,1:T(8,128)S(1)}) all-reduce(f32[32,32]{0,1:T(8,128)S(1)} %fusion.6, f32[32,32]{0,1:T(8,128)S(1)} %fusion.4), channel_id=1, replica_groups=mesh['rows'=8,'grp'=4] {'rows','grp'}, use_global_device_ids=true, to_apply=%region_9.14 | all-reduce | flops 2048 | bytes 16384 | tf_op jit(solution)/shard_map/psum | solution.py:51
  254.5 0.7 gather_fusion.3
  256.1 2.9 %cholesky.282 = f32[32,32]{1,0:T(8,128)S(1)} custom-call(f32[32,32]{1,0:T(8,128)S(1)} %fusion.103), custom_call_target="Cholesky" | custom-call | tf_op jit(solution)/shard_map/jit(cholesky)/cholesky | solution.py:38
  259.9 0.6 select_select_fusion.5
  260.8 0.7 copy.105
  261.8 2.9 %cholesky.293 = f32[32,32]{1,0:T(8,128)S(1)} custom-call(f32[32,32]{1,0:T(8,128)S(1)} %fusion.95), custom_call_target="Cholesky" | custom-call | tf_op jit(solution)/shard_map/jit(cholesky)/cholesky | solution.py:68
  265.4 0.7 select_bitcast_fusion
  266.0 2.4 custom-call.49
  269.0 2.9 %cholesky.304 = f32[32,32]{1,0:T(8,128)S(1)} custom-call(f32[32,32]{1,0:T(8,128)S(1)} %fusion.94), custom_call_target="Cholesky" | custom-call | tf_op jit(solution)/shard_map/jit(cholesky)/cholesky | solution.py:36
  272.6 0.7 fusion.67
  273.3 2.4 custom-call.48
  276.5 2.9 %cholesky.315 = f32[32,32]{1,0:T(8,128)S(1)} custom-call(f32[32,32]{1,0:T(8,128)S(1)} %fusion.88), custom_call_target="Cholesky" | custom-call | tf_op jit(solution)/shard_map/jit(cholesky)/cholesky | solution.py:38
  280.1 1.3 select_select_fusion.4
  282.5 1.1 convolution_add_fusion
  (154 shorter events, 29.5 us)
Async XLA Ops:
  0.6 6.4 %copy-start = (f32[32,2048]{1,0:T(8,128)S(1)}, f32[32,2048]{1,0:T(8,128)}, u32[]{:S(2)}) copy-start(f32[32,2048]{1,0:T(8,128)} %param.10) | copy-start | bytes 786436
  2.6 4.4 %copy-start.1 = (f32[32,32]{1,0:T(8,128)S(1)}, f32[32,32]{1,0:T(8,128)}, u32[]{:S(2)}) copy-start(f32[32,32]{1,0:T(8,128)} %param.11) | copy-start | bytes 12292
  2.6 9.0 %all-to-all-start = ((bf16[8,4,2048]{2,0,1:T(8,128)(2,1)}), bf16[8,4,2048]{2,0,1:T(8,128)(2,1)S(1)}, u32[]{:S(2)}, u32[]{:S(2)}) async-start(bf16[8,4,2048]{2,0,1:T(8,128)(2,1)} %bitcast), calls=%async_computation | async-start | bytes 262144 | tf_op jit(solution)/shard_map/all_to_all | solution.py:49
  11.6 64.9 %all-to-all-start.1 = ((bf16[8,4,2048]{2,0,1:T(8,128)(2,1)}), bf16[8,4,2048]{2,0,1:T(8,128)(2,1)S(1)}, u32[]{:S(2)}, u32[]{:S(2)}) async-start(bf16[8,4,2048]{2,0,1:T(8,128)(2,1)} %bitcast.15), calls=%async_computation.1 | async-start | bytes 262144 | tf_op jit(solution)/shard_map/all_to_all | solution.py:49
  76.5 69.2 %all-to-all-start.2 = ((bf16[8,4,2048]{2,0,1:T(8,128)(2,1)}), bf16[8,4,2048]{2,0,1:T(8,128)(2,1)S(1)}, u32[]{:S(2)}, u32[]{:S(2)}) async-start(bf16[8,4,2048]{2,0,1:T(8,128)(2,1)} %bitcast.39), calls=%async_computation.2 | async-start | bytes 262144 | tf_op jit(solution)/shard_map/all_to_all | solution.py:49
  145.7 68.5 %all-to-all-start.3 = ((bf16[8,4,2048]{2,0,1:T(8,128)(2,1)}), bf16[8,4,2048]{2,0,1:T(8,128)(2,1)S(1)}, u32[]{:S(2)}, u32[]{:S(2)}) async-start(bf16[8,4,2048]{2,0,1:T(8,128)(2,1)} %bitcast.63), calls=%async_computation.3 | async-start | bytes 262144 | tf_op jit(solution)/shard_map/all_to_all | solution.py:49
where the time goes:
time: 285 us; the launch traced here: 284 us
  blocking collectives  164 us (58%)
  other arithmetic  71.8 us (25%)
  matrix products  20.3 us (7%)
  starting transfers between devices  14.7 us (5%)
  local copies, waits for them, and re-layouts  7.12 us (2%)
  waiting for transfers between devices  4.15 us (1%)
    psum x3, blocking collectives, body(): lax.psum((contract_rows(basis_now, raw), contract_rows(raw, raw)), ('rows...  122 us
    psum x1, blocking collectives, body(): gram_basis = lax.psum(contract_rows(basis_now, basis_now), ('rows', 'grp'))  42.1 us
    another operation x16, other arithmetic, lower_solve(): lax.linalg.triangular_solve(factor, right, left_side=True, lower=True)  24.7 us
    all_to_all x4, starting transfers between devices, body(): lax.all_to_all(snapshots[batch], 'grp', split_axis=1, concat_axis=0, tile...  14.7 us
    another operation x12, other arithmetic, small_update(): jnp.linalg.cholesky(matmul(rotation.T, matmul(moment, rotation)))  14.7 us
    another operation x12, other arithmetic, small_update(): factor = jnp.linalg.cholesky(matmul(leading.T, leading))  14.4 us
    another operation x12, other arithmetic, body(): lower = jnp.linalg.cholesky(gram)  14.4 us
    dot_general x54, matrix products, matmul(): jnp.dot(left, right, precision=lax.Precision.HIGHEST, preferred_element_t...  13.7 us
  transfers between devices with their start and end apart: 4, of which 1 were waited for; matrix products, arithmetic and copies ran while one was open for 24% of the time, Pallas kernels for 0%

commit v1 on v0

--- a/solution.py
+++ b/solution.py
@@ -48,9 +48,12 @@
     for batch in range(BATCHES):
         columns = lax.all_to_all(snapshots[batch], "grp", split_axis=1, concat_axis=0, tiled=True)
         raw = columns.astype(jnp.float32)
-        raw_cross, raw_gram = lax.psum(
-            (contract_rows(basis_now, raw), contract_rows(raw, raw)), ("rows", "grp")
-        )
+
+        def review_racks(array_here):
+            front = lax.psum(lax.psum(array_here, "grp"), "rows")
+            return front
+
+        raw_cross, raw_gram = review_racks((contract_rows(basis_now, raw), contract_rows(raw, raw)))
         inverse = lax.rsqrt(jnp.diagonal(raw_gram) + epsilon)
         scaled = raw * inverse[:, None]
         cross = raw_cross * inverse[None, :]

time: 285 us -> 340 us (1.19)
  blocking collectives: 164 us -> 224 us
  waiting for transfers between devices: 4.15 us -> 0.01 us
    psum x3 -> x8, blocking collectives: 122 us -> 182 us  [review_racks(): front = lax.psum(lax.psum(array_here, 'grp'), 'rows')]
    all_to_all x4, waiting for transfers between devices: 4.15 us -> 0.01 us  [body(): lax.all_to_all(snapshots[batch], 'grp', split_axis=1, concat_axis=0, tile...]
  transfers between devices with their start and end apart: 4 -> 4, of which waited for: 1 -> 0; matrix products, arithmetic and copies ran while one was open for 24% -> 20% of each run, Pallas kernels for 0% -> 0%
where the time goes in v1:
time: 340 us; the launch traced here: 339 us
  blocking collectives  224 us (66%)
  other arithmetic  71.8 us (21%)
  matrix products  20.2 us (6%)
  starting transfers between devices  14.6 us (4%)
  local copies, waits for them, and re-layouts  7.11 us (2%)
    psum x8, blocking collectives, review_racks(): front = lax.psum(lax.psum(array_here, 'grp'), 'rows')  182 us
    psum x1, blocking collectives, body(): gram_basis = lax.psum(contract_rows(basis_now, basis_now), ('rows', 'grp'))  41.7 us
    another operation x16, other arithmetic, lower_solve(): lax.linalg.triangular_solve(factor, right, left_side=True, lower=True)  24.7 us
    another operation x12, other arithmetic, small_update(): jnp.linalg.cholesky(matmul(rotation.T, matmul(moment, rotation)))  14.7 us
    all_to_all x4, starting transfers between devices, body(): lax.all_to_all(snapshots[batch], 'grp', split_axis=1, concat_axis=0, tile...  14.6 us
    another operation x12, other arithmetic, small_update(): factor = jnp.linalg.cholesky(matmul(leading.T, leading))  14.4 us
    another operation x12, other arithmetic, body(): lower = jnp.linalg.cholesky(gram)  14.4 us
    dot_general x54, matrix products, matmul(): jnp.dot(left, right, precision=lax.Precision.HIGHEST, preferred_element_t...  13.7 us
  transfers between devices with their start and end apart: 4, of which 0 were waited for; matrix products, arithmetic and copies ran while one was open for 20% of the time, Pallas kernels for 0%

profile of v1, /device:TPU:0, one launch (start us, length us, event | category | flops | bytes accessed | tf_op | source)
XLA Modules:
  0.0 338.7 jit_solution(9093868644817619418)
XLA Ops:
  0.6 1.9 fusion.229
  2.6 4.4 %all-to-all-start = ((bf16[8,4,2048]{2,0,1:T(8,128)(2,1)}), bf16[8,4,2048]{2,0,1:T(8,128)(2,1)S(1)}, u32[]{:S(2)}, u32[]{:S(2)}) async-start(bf16[8,4,2048]{2,0,1:T(8,128)(2,1)} %bitcast), calls=%async_computation | async-start | bytes 262144 | tf_op jit(solution)/shard_map/all_to_all | solution.py:49
  7.4 41.7 %psum.123 = f32[32,32]{1,0:T(8,128)S(1)} all-reduce(f32[32,32]{1,0:T(8,128)S(1)} %fusion.230), channel_id=1, replica_groups=mesh['rows'=8,'grp'=4] {'rows','grp'}, use_global_device_ids=true, to_apply=%region_4.0 | all-reduce | flops 1024 | bytes 8192 | tf_op jit(solution)/shard_map/psum | solution.py:47
  49.1 3.6 %all-to-all-start.1 = ((bf16[8,4,2048]{2,0,1:T(8,128)(2,1)}), bf16[8,4,2048]{2,0,1:T(8,128)(2,1)S(1)}, u32[]{:S(2)}, u32[]{:S(2)}) async-start(bf16[8,4,2048]{2,0,1:T(8,128)(2,1)} %bitcast.15), calls=%async_computation.1 | async-start | bytes 262144 | tf_op jit(solution)/shard_map/all_to_all | solution.py:49
  53.1 11.9 %all-reduce.11 = (f32[32,32]{0,1:T(8,128)S(1)}, f32[32,32]{0,1:T(8,128)S(1)}) all-reduce(f32[32,32]{0,1:T(8,128)S(1)} %fusion.18, f32[32,32]{0,1:T(8,128)S(1)} %fusion.16), channel_id=1, replica_groups=mesh['rows'=8,'grp'=4] {'grp'}, use_global_device_ids=true, to_apply=%region_0.0 | all-reduce | flops 2048 | bytes 16384 | tf_op jit(solution)/shard_map/psum | solution.py:53
  65.0 36.5 %all-reduce.7 = (f32[32,32]{0,1:T(8,128)S(1)}, f32[32,32]{0,1:T(8,128)S(1)}) all-reduce(f32[32,32]{0,1:T(8,128)S(1)} %get-tuple-element.27, f32[32,32]{0,1:T(8,128)S(1)} %get-tuple-element.28), channel_id=1, replica_groups=mesh['rows'=8,'grp'=4] {'rows'}, use_global_device_ids=true, to_apply=%region_1.0 | all-reduce | flops 2048 | bytes 16384 | tf_op jit(solution)/shard_map/psum | solution.py:53
  101.5 0.7 gather_fusion
  103.5 2.9 cholesky.194
  107.1 0.7 fusion.143
  107.7 2.4 custom-call.34
  111.3 2.9 cholesky.205
  114.9 0.7 fusion.64
  115.6 2.4 custom-call.33
  120.6 3.3 all-to-all-start.2
  124.4 11.9 %all-reduce.10 = (f32[32,32]{0,1:T(8,128)S(1)}, f32[32,32]{0,1:T(8,128)S(1)}) all-reduce(f32[32,32]{0,1:T(8,128)S(1)} %fusion.14, f32[32,32]{0,1:T(8,128)S(1)} %fusion.12), channel_id=1, replica_groups=mesh['rows'=8,'grp'=4] {'grp'}, use_global_device_ids=true, to_apply=%region_7.11 | all-reduce | flops 2048 | bytes 16384 | tf_op jit(solution)/shard_map/psum | solution.py:53
  136.3 33.1 %all-reduce.6 = (f32[32,32]{0,1:T(8,128)S(1)}, f32[32,32]{0,1:T(8,128)S(1)}) all-reduce(f32[32,32]{0,1:T(8,128)S(1)} %get-tuple-element.25, f32[32,32]{0,1:T(8,128)S(1)} %get-tuple-element.26), channel_id=1, replica_groups=mesh['rows'=8,'grp'=4] {'rows'}, use_global_device_ids=true, to_apply=%region_8.12 | all-reduce | flops 2048 | bytes 16384 | tf_op jit(solution)/shard_map/psum | solution.py:53
  169.4 0.7 gather_fusion.1
  170.9 2.9 cholesky.216
  175.9 2.9 cholesky.227
  179.5 0.7 fusion.144
  180.2 2.4 custom-call.39
  183.8 2.9 cholesky.238
  187.4 0.7 fusion.65
  188.1 2.4 custom-call.38
  193.1 3.3 all-to-all-start.3
  196.9 11.9 %all-reduce.9 = (f32[32,32]{0,1:T(8,128)S(1)}, f32[32,32]{0,1:T(8,128)S(1)}) all-reduce(f32[32,32]{0,1:T(8,128)S(1)} %fusion.10, f32[32,32]{0,1:T(8,128)S(1)} %fusion.8), channel_id=1, replica_groups=mesh['rows'=8,'grp'=4] {'grp'}, use_global_device_ids=true, to_apply=%region_11.16 | all-reduce | flops 2048 | bytes 16384 | tf_op jit(solution)/shard_map/psum | solution.py:53
  208.8 33.2 %all-reduce.5 = (f32[32,32]{0,1:T(8,128)S(1)}, f32[32,32]{0,1:T(8,128)S(1)}) all-reduce(f32[32,32]{0,1:T(8,128)S(1)} %get-tuple-element.23, f32[32,32]{0,1:T(8,128)S(1)} %get-tuple-element.24), channel_id=1, replica_groups=mesh['rows'=8,'grp'=4] {'rows'}, use_global_device_ids=true, to_apply=%region_12.17 | all-reduce | flops 2048 | bytes 16384 | tf_op jit(solution)/shard_map/psum | solution.py:53
  242.0 0.7 gather_fusion.2
  243.6 2.9 cholesky.249
  248.6 2.9 cholesky.260
  252.2 0.7 fusion.142
  252.9 2.4 custom-call.44
  256.5 2.9 cholesky.271
  260.1 0.7 fusion.66
  260.7 2.4 custom-call.43
  266.2 10.3 %all-reduce.8 = (f32[32,32]{0,1:T(8,128)S(1)}, f32[32,32]{0,1:T(8,128)S(1)}) all-reduce(f32[32,32]{0,1:T(8,128)S(1)} %fusion.6, f32[32,32]{0,1:T(8,128)S(1)} %fusion.4), channel_id=1, replica_groups=mesh['rows'=8,'grp'=4] {'grp'}, use_global_device_ids=true, to_apply=%region_15.20 | all-reduce | flops 2048 | bytes 16384 | tf_op jit(solution)/shard_map/psum | solution.py:53
  276.5 33.1 %all-reduce.4 = (f32[32,32]{0,1:T(8,128)S(1)}, f32[32,32]{0,1:T(8,128)S(1)}) all-reduce(f32[32,32]{0,1:T(8,128)S(1)} %get-tuple-element.21, f32[32,32]{0,1:T(8,128)S(1)} %get-tuple-element.22), channel_id=1, replica_groups=mesh['rows'=8,'grp'=4] {'rows'}, use_global_device_ids=true, to_apply=%region_16.21 | all-reduce | flops 2048 | bytes 16384 | tf_op jit(solution)/shard_map/psum | solution.py:53
  309.6 0.7 gather_fusion.3
  311.2 2.9 cholesky.282
  315.9 0.7 copy.105
  316.9 2.9 cholesky.293
  320.5 0.7 select_bitcast_fusion
  321.1 2.4 custom-call.49
  324.2 2.9 cholesky.304
  328.4 2.4 custom-call.48
  331.6 2.9 cholesky.315
  335.2 1.3 select_select_fusion.4
  337.6 1.1 convolution_add_fusion
  (159 shorter events, 32.1 us)
Async XLA Ops:
  0.6 6.4 %copy-start = (f32[32,2048]{1,0:T(8,128)S(1)}, f32[32,2048]{1,0:T(8,128)}, u32[]{:S(2)}) copy-start(f32[32,2048]{1,0:T(8,128)} %param.10) | copy-start | bytes 786436
  2.6 4.4 %copy-start.1 = (f32[32,32]{1,0:T(8,128)S(1)}, f32[32,32]{1,0:T(8,128)}, u32[]{:S(2)}) copy-start(f32[32,32]{1,0:T(8,128)} %param.11) | copy-start | bytes 12292
  2.6 46.5 %all-to-all-start = ((bf16[8,4,2048]{2,0,1:T(8,128)(2,1)}), bf16[8,4,2048]{2,0,1:T(8,128)(2,1)S(1)}, u32[]{:S(2)}, u32[]{:S(2)}) async-start(bf16[8,4,2048]{2,0,1:T(8,128)(2,1)} %bitcast), calls=%async_computation | async-start | bytes 262144 | tf_op jit(solution)/shard_map/all_to_all | solution.py:49
  49.1 71.6 %all-to-all-start.1 = ((bf16[8,4,2048]{2,0,1:T(8,128)(2,1)}), bf16[8,4,2048]{2,0,1:T(8,128)(2,1)S(1)}, u32[]{:S(2)}, u32[]{:S(2)}) async-start(bf16[8,4,2048]{2,0,1:T(8,128)(2,1)} %bitcast.15), calls=%async_computation.1 | async-start | bytes 262144 | tf_op jit(solution)/shard_map/all_to_all | solution.py:49
  120.6 72.5 %all-to-all-start.2 = ((bf16[8,4,2048]{2,0,1:T(8,128)(2,1)}), bf16[8,4,2048]{2,0,1:T(8,128)(2,1)S(1)}, u32[]{:S(2)}, u32[]{:S(2)}) async-start(bf16[8,4,2048]{2,0,1:T(8,128)(2,1)} %bitcast.39), calls=%async_computation.2 | async-start | bytes 262144 | tf_op jit(solution)/shard_map/all_to_all | solution.py:49
  193.1 72.7 %all-to-all-start.3 = ((bf16[8,4,2048]{2,0,1:T(8,128)(2,1)}), bf16[8,4,2048]{2,0,1:T(8,128)(2,1)S(1)}, u32[]{:S(2)}, u32[]{:S(2)}) async-start(bf16[8,4,2048]{2,0,1:T(8,128)(2,1)} %bitcast.63), calls=%async_computation.3 | async-start | bytes 262144 | tf_op jit(solution)/shard_map/all_to_all | solution.py:49
